TPU v7x, 32 devices: a whole 2x2x4 slice. The times are simulated.
32 devices in a mesh: ens: 2 (over y), box: 4 (over z), slab: 4 (over x, core).
Axes of the slice: x: 2, y: 2, z: 4, core: 2. Of those that a mesh axis runs over, the one named last changes fastest.
Arguments:
- pressure_now: float32 [4, 64, 64, 256], P('ens', 'box', 'slab'), parts along dimension 0, may hold values from -6 to 6
- pressure_prev: float32 [4, 64, 64, 256], P('ens', 'box', 'slab'), parts along dimension 0, may hold values from -6 to 6
- courant_sq: float32 [64, 64, 256], P('box', 'slab'), may hold values from 0.04 to 0.28
- member_profiles: float32 [8, 64], replicated, may hold values from -0.15 to 0.15
- member_ids: int32 [4], P('ens'), parts along dimension 0, may hold values from 0 to 7, as said below
- stored_slabs: float32 [8, 16, 6144], P('slab'), may hold values from -6 to 6
- slab_home: int32 [2], P('ens'), parts along dimension 0, may hold values from 0 to 7
- interp_weights: float32 [2, 16], replicated, may hold values from -1.5 to 1.5
- surface_cells: int32 [6, 1024], replicated, may hold values from 0 to 1048575, as said below
Outputs:
- pressure_next: float32 [4, 64, 64, 256], P('ens', 'box', 'slab'), parts along dimension 0
- pressure_last: float32 [4, 64, 64, 256], P('ens', 'box', 'slab'), parts along dimension 0
There are 2 independent parts, one for each index of `ens`. A program takes and returns all parts, laid end to end along the dimension named above; an argument that names none is the same for every part. Nothing has to cross between parts.
Inputs may be any that keep to these rules, and one draw needn't show every extreme that they name: `surface_cells`: row f lists 1024 cells, flat index (x 64 + z) * 256 + y, on one face of the box surface 0 cells inside the grid: x low, x high, z low, z high, y low, y high in this order; the other two coordinates lie on the surface; on every face other than the two depth faces, every depth of the surface occurs; cells may repeat. `slab_home`: block k is stored on the slab device k // 2, in its slot k % 2. `member_ids`: the members' profiles are all different.
All inputs are finite; a program needn't handle non-finite values.
Results may differ from a plain program's by a relative error of at most 0.000098.
Values sent between devices are 32-bit elements; how exact they have to be, the bound alone decides.
A program may use at most 64 MiB of HBM per device.

v0:
```python
import functools

import jax
import jax.numpy as jnp
from jax import lax
from jax.experimental import pallas as pl
from jax.experimental.pallas import tpu as pltpu
from jax.sharding import PartitionSpec as P

F32, BF16, I32 = jnp.float32, jnp.bfloat16, jnp.int32
MESH = pl.DeviceIdType.MESH


def iota(shape, dim):
    return lax.broadcasted_iota(I32, shape, dim)


def quotient(values, divisor):
    if divisor & (divisor - 1) == 0:
        return lax.shift_right_logical(values, divisor.bit_length() - 1)
    return lax.div(values, jnp.full_like(values, divisor))


def split3(v):
    high = v.astype(BF16).astype(F32)
    rest = v - high
    mid = rest.astype(BF16).astype(F32)
    return high, mid, rest - mid


def place(rows, row_of, valid, per_step, right):
    hit = (iota((rows, row_of.shape[1]), 0) == row_of) & valid
    parts = []
    for v in per_step:
        for term in split3(v):
            parts.append(jnp.where(hit, term, 0.0).astype(BF16))
    left = jnp.concatenate(parts, axis=0)
    sums = lax.dot_general(left, right, (((1,), (1,)), ((), ())), preferred_element_type=F32)
    out = []
    for t in range(len(per_step)):
        a = sums[3 * t * rows : (3 * t + 1) * rows]
        b = sums[(3 * t + 1) * rows : (3 * t + 2) * rows]
        c = sums[(3 * t + 2) * rows : (3 * t + 3) * rows]
        out.append(a + (b + c))
    return out


def kernel(dims, home, ids_h, prof_h, weights_h, cells_h, now_h, prev_h, cour_h, slabs_h, two, one,
           ids, prof, weights, cells, now, prev, coef, slabs, xsend, zsend, xghost, zghost, xextra, zextra,
           hot_x, hot_z, hot_low, hot_high, vsend, vrecv, load_sem, hs_sem, hr_sem, vs_sem, vr_sem):
    members, wx, wz, ny, slots, length, pts, n_box, n_slab = dims
    steps = 2
    block = wx * wz
    box, slab = lax.axis_index("box"), lax.axis_index("slab")
    pairs = ((now_h, now), (slabs_h, slabs), (weights_h, weights), (cour_h, coef.at[pl.ds(0, block)]),
             (prof_h, prof), (ids_h, ids), (prev_h, prev), (cells_h, cells))
    loads = [pltpu.make_async_copy(src, dst, load_sem.at[i]) for i, (src, dst) in enumerate(pairs)]
    loads[0].start()

    barrier = pltpu.get_barrier_semaphore()

    def greet(target):
        pl.semaphore_signal(barrier, inc=1, device_id=target, device_id_type=MESH)

    @pl.when(box > 0)
    def _():
        greet({"box": box - 1})

    @pl.when(box < n_box - 1)
    def _():
        greet({"box": box + 1})

    for d in range(1, n_slab):
        greet({"slab": lax.rem(slab + d, n_slab)})
    for c in loads[1:]:
        c.start()

    def source(r, way, m):
        if r > 0:
            return xsend.at[way, m]
        return now.at[pl.ds((m * wx + (wx - 1 if way == 0 else 0)) * wz, wz)]

    def halo(r, way):
        if way < 2:
            peer = {"box": box + 1 if way == 0 else box - 1}
            return [
                pltpu.make_async_remote_copy(
                    source(r, way, m), xghost.at[r, way, m],
                    hs_sem.at[r, way, m], hr_sem.at[r, way, m], device_id=peer, device_id_type=MESH)
                for m in range(members)
            ]
        peer = {"slab": slab + 1 if way == 2 else slab - 1}
        return [
            pltpu.make_async_remote_copy(
                zsend.at[r, way - 2], zghost.at[r, way - 2], hs_sem.at[r, way, 0], hr_sem.at[r, way, 0],
                device_id=peer, device_id_type=MESH)
        ]

    sends_to = (box < n_box - 1, box > 0, slab < n_slab - 1, slab > 0)
    hears_from = (box > 0, box < n_box - 1, slab > 0, slab < n_slab - 1)

    def pack(field, r):
        for m in range(members):
            if r > 0:
                for way in (0, 1):
                    plane = wx - 1 if way == 0 else 0
                    xsend[way, m] = field[pl.ds((m * wx + plane) * wz, wz), :]
            for way in (2, 3):
                row = wz - 1 if way == 2 else 0
                for x in range(wx):
                    zsend[r, way - 2, m, x : x + 1, :] = field[pl.ds((m * wx + x) * wz + row, 1), :]

    def send_halos(r):
        for way in range(4):
            @pl.when(sends_to[way])
            def _(way=way):
                for c in halo(r, way):
                    c.start()

    def add_halos(r, out):
        for way in (0, 1):
            plane = 0 if way == 0 else wx - 1

            @pl.when(hears_from[way])
            def _(way=way, plane=plane):
                for m, c in enumerate(halo(r, way)):
                    c.wait_recv()
                for m in range(members):
                    rows = pl.ds((m * wx + plane) * wz, wz)
                    ghost = xghost[r, way, m]
                    if r > 0:
                        ghost = ghost + xextra[way]
                    out[rows, :] += coef[rows, :] * ghost
        for way in (2, 3):
            row = 0 if way == 2 else wz - 1

            @pl.when(hears_from[way])
            def _(way=way, row=row):
                for c in halo(r, way):
                    c.wait_recv()
                for m in range(members):
                    for x in range(wx):
                        at = pl.ds((m * wx + x) * wz + row, 1)
                        ghost = zghost[r, way - 2, m, x : x + 1, :]
                        if r > 0:
                            ghost = ghost + zextra[way - 2, x : x + 1, :]
                        out[at, :] += coef[at, :] * ghost

    def end_sends(r):
        for way in range(4):
            @pl.when(sends_to[way])
            def _(way=way):
                for c in halo(r, way):
                    c.wait_send()

    loads[0].wait()
    pack(now, 0)
    box_peers = jnp.where(box > 0, 1, 0) + jnp.where(box < n_box - 1, 1, 0)
    pl.semaphore_wait(barrier, n_slab - 1 + box_peers)
    send_halos(0)

    for i in (1, 2):
        loads[i].wait()
    eye = iota((length, length), 0) == iota((length, length), 1)
    cols = []
    for t in range(steps):
        col = jnp.sum(jnp.where(eye, weights[t : t + 1, :], 0.0), axis=1, keepdims=True)
        cols.append([jnp.where(home[0] == slab * slots + s, col, 0.0) for s in range(slots)])

    def offered(face, t):
        at = pl.ds(pl.multiple_of(face * pts, 128), pts)
        total = cols[t][0] * slabs[pl.ds(0, length), at]
        for s in range(1, slots):
            total = total + cols[t][s] * slabs[pl.ds(s * length, length), at]
        return jnp.sum(total, axis=0, keepdims=True)

    face_x = jnp.where(box == 0, 0, 1)
    face_z = jnp.where(slab == 0, 2, 3)
    common = [offered(f, t) for f in (face_x, 4, 5) for t in range(steps)]
    for kind in range(2):
        vsend[kind] = jnp.concatenate(common + [offered(2 + kind, t) for t in range(steps)], axis=0)

    def give(d):
        peer = lax.rem(slab + d, n_slab)
        return pltpu.make_async_remote_copy(
            vsend.at[jnp.where(peer == 0, 0, 1)], vrecv.at[d - 1], vs_sem.at[d - 1], vr_sem.at[d - 1],
            device_id={"slab": peer}, device_id_type=MESH)

    for d in range(1, n_slab):
        give(d).start()

    for i in (3, 4, 5):
        loads[i].wait()
    bank, total_z = prof.shape
    here = iota((wz, total_z), 1) == slab * wz + iota((wz, total_z), 0)
    for m in reversed(range(members)):
        mine = jnp.sum(jnp.where(iota((bank, total_z), 0) == ids[m], prof[...], 0.0), axis=0, keepdims=True)
        gain = 1.0 + jnp.sum(jnp.where(here, mine, 0.0), axis=1, keepdims=True)
        for x in range(wx):
            coef[pl.ds((m * wx + x) * wz, wz), :] = coef[pl.ds(x * wz, wz), :] * gain

    z_at, y_at = iota((wz, ny), 0), iota((wz, ny), 1)

    def advance(field, before, out):
        def member(m, carry):
            base = m * block
            for x in range(wx):
                rows = pl.ds(pl.multiple_of(base + x * wz, 8), wz)
                c = field[rows, :]
                lap = -6.0 * c
                if x > 0:
                    lap = lap + field[pl.ds(pl.multiple_of(base + (x - 1) * wz, 8), wz), :]
                if x < wx - 1:
                    lap = lap + field[pl.ds(pl.multiple_of(base + (x + 1) * wz, 8), wz), :]
                lap = lap + jnp.where(z_at == 0, 0.0, pltpu.roll(c, 1, 0))
                lap = lap + jnp.where(z_at == wz - 1, 0.0, pltpu.roll(c, wz - 1, 0))
                lap = lap + jnp.where(y_at == 0, 0.0, pltpu.roll(c, 1, 1))
                lap = lap + jnp.where(y_at == ny - 1, 0.0, pltpu.roll(c, ny - 1, 1))
                out[rows, :] = (2.0 * c - before[rows, :]) + coef[rows, :] * lap
            return carry

        lax.fori_loop(0, members, member, 0)

    loads[6].wait()
    advance(now, prev, one)

    loads[7].wait()
    margin, wide = 8, 128

    def where_is(face):
        cell = cells[pl.ds(face, 1), :]
        cx = quotient(cell, total_z * ny)
        rest = cell - cx * (total_z * ny)
        cz = quotient(rest, ny)
        return cx - box * wx, cz - slab * wz, rest - cz * ny

    def hot(cols, col_of):
        return jnp.where(iota((cols, pts), 0) == col_of, 1.0, 0.0).astype(BF16)

    px, pz, py = where_is(face_x)
    px_valid = (px >= 0) & (px < wx)
    px_row = pz + margin
    hot_x[...] = hot(ny, py)
    px, pz, py = where_is(face_z)
    pz_valid = (pz >= 0) & (pz < wz)
    pz_row = px + margin
    hot_z[...] = hot(ny, py)
    px, pz, py = where_is(4)
    low_row = pz + margin
    hot_low[...] = hot(wide, px + margin)
    px, pz, py = where_is(5)
    high_row = pz + margin
    hot_high[...] = hot(wide, px + margin)

    add_halos(0, one)
    pack(one, 1)
    send_halos(1)

    for d in range(1, n_slab):
        give(d).wait_recv()
    values = vsend[jnp.where(slab == 0, 0, 1)]
    for d in range(1, n_slab):
        values = values + vrecv[d - 1]

    def rows_of(k):
        return [values[2 * k + t : 2 * k + t + 1] for t in range(steps)]

    tall_x, tall_z = wx + 2 * margin, wz + 2 * margin
    always = low_row >= -tall_z * n_slab * pts
    on_x = place(tall_z, px_row, px_valid, rows_of(0), hot_x[...])
    on_z = place(tall_x, pz_row, pz_valid, rows_of(3), hot_z[...])
    low_y = place(tall_z, low_row, always, rows_of(1), hot_low[...])
    high_y = place(tall_z, high_row, always, rows_of(2), hot_high[...])
    plane_x = jnp.where(box == 0, 0, wx - 1)
    row_z = jnp.where(slab == 0, 0, wz - 1) + margin
    tall_row, tall_lane = iota((tall_z, ny), 0), iota((tall_z, ny), 1)

    def source_plane(t, x):
        at = x + margin
        out = jnp.where(tall_row == row_z, on_z[t][at : at + 1, :], 0.0)
        out = out + jnp.where(tall_lane == 0, low_y[t][:, at : at + 1], 0.0)
        out = out + jnp.where(tall_lane == ny - 1, high_y[t][:, at : at + 1], 0.0)
        if x in (0, wx - 1):
            out = out + jnp.where(plane_x == x, on_x[t], 0.0)
        return out

    def add_source(t, out):
        for x in range(wx):
            plane = source_plane(t, x)
            if t == 0:
                zextra[0, x : x + 1, :] = plane[margin - 1 : margin]
                zextra[1, x : x + 1, :] = plane[margin + wz : margin + wz + 1]
            for m in range(members):
                out[pl.ds((m * wx + x) * wz, wz), :] += plane[margin : margin + wz]
        if t == 0:
            xextra[0] = source_plane(t, -1)[margin : margin + wz]
            xextra[1] = source_plane(t, wx)[margin : margin + wz]

    add_source(0, one)
    advance(one, now, two)
    add_source(1, two)
    add_halos(1, two)
    end_sends(0)
    end_sends(1)
    for d in range(1, n_slab):
        give(d).wait_send()


def store_kernel(two, one, next_h, last_h, sem):
    copies = [pltpu.make_async_copy(src, dst, sem.at[i]) for i, (src, dst) in enumerate(((two, next_h), (one, last_h)))]
    for c in copies:
        c.start()
    for c in copies:
        c.wait()


def on_device(pressure_now, pressure_prev, courant_sq, member_profiles, member_ids, stored_slabs,
              slab_home, interp_weights, surface_cells):
    members, wx, wz, ny = pressure_now.shape
    slots, length, points = stored_slabs.shape
    pts = surface_cells.shape[1]
    n_box, n_slab = lax.axis_size("box"), lax.axis_size("slab")
    dims = (members, wx, wz, ny, slots, length, pts, n_box, n_slab)
    rows = members * wx * wz
    vmem = pl.BlockSpec(memory_space=pltpu.VMEM)
    in_hbm = lambda a: pltpu.with_memory_space_constraint(a, pltpu.HBM)
    hbm = pl.BlockSpec(memory_space=pltpu.HBM)
    field = jax.ShapeDtypeStruct((rows, ny), F32)
    dma = pltpu.SemaphoreType.DMA
    new, last = pl.pallas_call(
        functools.partial(kernel, dims),
        out_shape=(field, field),
        in_specs=[pl.BlockSpec(memory_space=pltpu.SMEM)] + [hbm] * 8,
        out_specs=(vmem, vmem),
        scratch_shapes=[
            pltpu.SMEM(member_ids.shape, I32),
            pltpu.VMEM(member_profiles.shape, F32), pltpu.VMEM(interp_weights.shape, F32),
            pltpu.VMEM(surface_cells.shape, I32),
            pltpu.VMEM((rows, ny), F32), pltpu.VMEM((rows, ny), F32), pltpu.VMEM((rows, ny), F32),
            pltpu.VMEM((slots * length, points), F32),
            pltpu.VMEM((2, members, wz, ny), F32),
            pltpu.VMEM((2, 2, members, wx, ny), F32),
            pltpu.VMEM((2, 2, members, wz, ny), F32),
            pltpu.VMEM((2, 2, members, wx, ny), F32),
            pltpu.VMEM((2, wz, ny), F32), pltpu.VMEM((2, wx, ny), F32),
            pltpu.VMEM((ny, pts), BF16), pltpu.VMEM((ny, pts), BF16),
            pltpu.VMEM((128, pts), BF16), pltpu.VMEM((128, pts), BF16),
            pltpu.VMEM((2, 8, pts), F32),
            pltpu.VMEM((n_slab - 1, 8, pts), F32),
            dma((8,)), dma((2, 4, members)), dma((2, 4, members)),
            dma((n_slab - 1,)), dma((n_slab - 1,)),
        ],
        compiler_params=pltpu.CompilerParams(collective_id=0, has_side_effects=True,
                                             vmem_limit_bytes=32 * 1024 * 1024),
    )(slab_home, *(in_hbm(a) for a in (
        member_ids, member_profiles, interp_weights, surface_cells,
        pressure_now.reshape(rows, ny), pressure_prev.reshape(rows, ny),
        courant_sq.reshape(wx * wz, ny), stored_slabs.reshape(slots * length, points),
    )))
    placed = pltpu.HBM((rows, ny), F32)
    new, last = pl.pallas_call(
        store_kernel,
        out_shape=(placed, placed),
        in_specs=[vmem, vmem],
        out_specs=(hbm, hbm),
        scratch_shapes=[dma((2,))],
        compiler_params=pltpu.CompilerParams(vmem_limit_bytes=4 * 1024 * 1024),
    )(new, last)
    return new.reshape(pressure_now.shape), last.reshape(pressure_now.shape)


def solution(mesh):
    in_specs = (
        P("ens", "box", "slab", None), P("ens", "box", "slab", None), P("box", "slab", None), P(),
        P("ens"), P("slab", None, None), P("ens"), P(), P(),
    )
    out_specs = (P("ens", "box", "slab", None), P("ens", "box", "slab", None))
    return jax.shard_map(on_device, mesh=mesh, in_specs=in_specs, out_specs=out_specs, check_vma=False)
```

profile of v0, /device:TPU:0, one launch (start us, length us, event | category | flops | bytes accessed | tf_op | source)
XLA Modules:
  0.0 12.9 jit_solution(13516608304437720889)
XLA Ops:
  1.3 10.6 %shard_map.104 = (f32[512,256]{1,0:T(8,128)S(1)}, f32[512,256]{1,0:T(8,128)S(1)}) custom-call(s32[1]{0:T(128)S(6)} %copy.11.home, s32[2]{0:T(128)} %ids_h.1, f32[8,64]{1,0:T(8,128)} %prof_h.1, f32[2,16]{1,0:T(2,128)} %weights_h.1, s32[6,1024]{1,0:T(8,128)} %cells_h.1, f32[512,256]{1,0:T(8,128)} %bitcast.7, f32[512,256]{1,0:T(8,128)} %bitcast.8, ...), custom_call_target="tpu_custom_call" | custom-call | tf_op jit(solution)/shard_map/pallas_call | solution.py:330
  11.9 1.0 %shard_map.105 = (f32[512,256]{1,0:T(8,128)}, f32[512,256]{1,0:T(8,128)}) custom-call(f32[512,256]{1,0:T(8,128)S(1)} %get-tuple-element.6.two, f32[512,256]{1,0:T(8,128)S(1)} %get-tuple-element.7.one), custom_call_target="tpu_custom_call" | custom-call | tf_op jit(solution)/shard_map/pallas_call | solution.py:361
where the time goes:
time: 13 us; the launch traced here: 12.9 us
  Pallas kernels  11.6 us (89%)
  between operations  1.29 us (10%)
    pallas_call x1, Pallas kernels, on_device(): pl.pallas_call(functools.partial(kernel, dims), out_shape=(field, field),...  10.6 us
    pallas_call x1, Pallas kernels, on_device(): pl.pallas_call(store_kernel, out_shape=(placed, placed), in_specs=[vmem,...  0.99 us

commit v1 on v0

v1 whole, which is shorter than its diff:
```python
import functools

import jax
import jax.numpy as jnp
from jax import lax
from jax.experimental import pallas as pl
from jax.experimental.pallas import tpu as pltpu
from jax.sharding import PartitionSpec as P

F32, BF16, I32 = jnp.float32, jnp.bfloat16, jnp.int32
MESH = pl.DeviceIdType.MESH
MARGIN, WIDE = 8, 128


def iota(shape, dim):
    return lax.broadcasted_iota(I32, shape, dim)


def quotient(values, divisor):
    if divisor & (divisor - 1) == 0:
        return lax.shift_right_logical(values, divisor.bit_length() - 1)
    return lax.div(values, jnp.full_like(values, divisor))


def split2(v):
    high = v.astype(BF16).astype(F32)
    return high, v - high


def place(row_hot, values, right):
    rows = row_hot.shape[0]
    parts = []
    for v in values:
        for term in split2(v):
            wide = jnp.broadcast_to(term, (16, v.shape[1])).astype(BF16)
            parts += [row_hot[r : r + 16, :] * wide for r in range(0, rows, 16)]
    left = jnp.concatenate(parts, axis=0)
    sums = lax.dot_general(left, right[...], (((1,), (1,)), ((), ())), preferred_element_type=F32)
    return [sums[2 * t * rows : (2 * t + 1) * rows] + sums[(2 * t + 1) * rows : (2 * t + 2) * rows]
            for t in range(len(values))]


def along_y(c, y_at):
    ny = c.shape[1]
    return (jnp.where(y_at == 0, 0.0, pltpu.roll(c, 1, 1))
            + jnp.where(y_at == ny - 1, 0.0, pltpu.roll(c, ny - 1, 1)))


def kernel(dims, home, ids_h, prof_h, weights_h, cells_h, now_h, prev_h, cour_h, slabs_h,
           one, now, coef, xout, zout, src,
           ids, prof, weights, cells, prev, cour, slab_y, slab_z, slab_x,
           psend, zsend, zpsend, csend, xghost, xcour, xpart, zghost, zpart, corner,
           row_x, row_z, row_low, row_high, hot_x, hot_z, hot_low, hot_high,
           ysend, xvsend, zvsend, yrecv, xvrecv, zvrecv,
           load_sem, hs_sem, hr_sem, cs_sem, cr_sem, vs_sem, vr_sem, diag_sem):
    members, wx, wz, ny, slots, length, pts, n_box, n_slab = dims
    steps = 2
    block = wx * wz
    box, slab = lax.axis_index("box"), lax.axis_index("slab")
    face_x = jnp.where(box == 0, 0, 1)
    box_edge = (box == 0) | (box == n_box - 1)
    slab_edge = (slab == 0) | (slab == n_slab - 1)
    pairs = (
        (slabs_h.at[:, pl.ds(4 * pts, 2 * pts)], slab_y), (weights_h, weights),
        (slabs_h.at[:, pl.ds(2 * pts, 2 * pts)], slab_z),
        (slabs_h.at[:, pl.ds(pl.multiple_of(face_x * pts, 128), pts)], slab_x),
        (now_h, now), (cour_h, cour), (prof_h, prof), (ids_h, ids), (prev_h, prev), (cells_h, cells))
    loads = [pltpu.make_async_copy(src_, dst, load_sem.at[i]) for i, (src_, dst) in enumerate(pairs)]
    for c in loads[:4]:
        c.start()

    barrier = pltpu.get_barrier_semaphore()

    def greet(target):
        pl.semaphore_signal(barrier, inc=1, device_id=target, device_id_type=MESH)

    sends_box = (box < n_box - 1, box > 0)
    sends_slab = (slab < n_slab - 1, slab > 0)
    hears_box = (box > 0, box < n_box - 1)
    hears_slab = (slab > 0, slab < n_slab - 1)
    shift = (1, -1)

    for d in range(1, n_slab):
        greet({"slab": lax.rem(slab + d, n_slab)})
    for a in range(2):
        @pl.when(sends_box[a])
        def _(a=a):
            greet({"box": box + shift[a]})
    for c in loads[4:]:
        c.start()

    for i in range(4):
        loads[i].wait()
    eye = iota((length, length), 0) == iota((length, length), 1)
    cols = []
    for t in range(steps):
        col = jnp.sum(jnp.where(eye, weights[t : t + 1, :], 0.0), axis=1, keepdims=True)
        cols.append([jnp.where(home[0] == slab * slots + s, col, 0.0) for s in range(slots)])

    def offered(ref, at, t):
        where = pl.ds(at, pts)
        total = cols[t][0] * ref[pl.ds(0, length), where]
        for s in range(1, slots):
            total = total + cols[t][s] * ref[pl.ds(s * length, length), where]
        return jnp.sum(total, axis=0, keepdims=True)

    both = range(steps)
    ysend[...] = jnp.concatenate([offered(slab_y, f * pts, t) for f in range(2) for t in both], axis=0)
    for f in range(2):
        zvsend[f] = jnp.concatenate([offered(slab_z, f * pts, t) for t in both], axis=0)
    xvsend[...] = jnp.concatenate([offered(slab_x, 0, t) for t in both], axis=0)

    loads[4].wait()
    loads[5].wait()
    edge_x, edge_z = (wx - 1, 0), (wz - 1, 0)
    for b in range(2):
        for x in range(wx):
            for m in range(members):
                zsend[b, m, x : x + 1, :] = now[pl.ds((m * wx + x) * wz + edge_z[b], 1), :]
            zsend[b, members, x : x + 1, :] = cour[pl.ds(x * wz + edge_z[b], 1), :]
        for a in range(2):
            for m in range(members):
                csend[a, b, m : m + 1, :] = now[pl.ds((m * wx + edge_x[a]) * wz + edge_z[b], 1), :]

    def give(d, kind):
        peer = lax.rem(slab + d, n_slab)
        ref, into = ((ysend, yrecv), (xvsend, xvrecv), (zvsend.at[0], zvrecv), (zvsend.at[1], zvrecv))[kind]
        k = min(kind, 2)
        return pltpu.make_async_remote_copy(
            ref, into.at[d - 1], vs_sem.at[d - 1, k], vr_sem.at[d - 1, k],
            device_id={"slab": peer}, device_id_type=MESH)

    def gives(d, kind):
        peer = lax.rem(slab + d, n_slab)
        return (None, box_edge, peer == 0, peer == n_slab - 1)[kind]

    def each_give(act):
        for d in range(1, n_slab):
            for kind in range(4):
                cond = gives(d, kind)
                if cond is None:
                    act(give(d, kind))
                else:
                    @pl.when(cond)
                    def _(d=d, kind=kind):
                        act(give(d, kind))

    given, parts = range(members + 1), range(members + 1, members + 2)

    def x_copies(a, which):
        peer = {"box": box + shift[a]}
        refs = [(now.at[pl.ds((m * wx + edge_x[a]) * wz, wz)], xghost.at[a, m]) for m in range(members)]
        refs += [(cour.at[pl.ds(edge_x[a] * wz, wz)], xcour.at[a]), (psend.at[a], xpart.at[a])]
        return [pltpu.make_async_remote_copy(*refs[i], hs_sem.at[a, i], hr_sem.at[a, i], device_id=peer, device_id_type=MESH)
                for i in which]

    def z_copy(b, i):
        source_, target = ((zsend.at[b], zghost.at[b]), (zpsend.at[b], zpart.at[b]))[i]
        return pltpu.make_async_remote_copy(source_, target, hs_sem.at[2 + b, i], hr_sem.at[2 + b, i],
                                            device_id={"slab": slab + shift[b]}, device_id_type=MESH)

    def corner_copy(a, b):
        return pltpu.make_async_remote_copy(
            csend.at[a, b], corner.at[a, b], cs_sem.at[a, b], cr_sem.at[a, b],
            device_id={"box": box + shift[a], "slab": slab + shift[b]}, device_id_type=MESH)

    box_peers = jnp.where(box > 0, 1, 0) + jnp.where(box < n_box - 1, 1, 0)
    pl.semaphore_wait(barrier, n_slab - 1 + box_peers)
    for a in range(2):
        @pl.when(sends_box[a])
        def _(a=a):
            pl.semaphore_signal(diag_sem.at[a], inc=1, device_id={"box": box + shift[a]}, device_id_type=MESH)
            for c in x_copies(a, given):
                c.start()
    each_give(lambda c: c.start())
    for b in range(2):
        @pl.when(sends_slab[b])
        def _(b=b):
            z_copy(b, 0).start()

    loads[6].wait()
    loads[7].wait()
    bank, total_z = prof.shape
    here = iota((wz, total_z), 1) == slab * wz + iota((wz, total_z), 0)
    beyond = [iota((1, total_z), 1) == slab * wz + at for at in (-1, wz)]
    gains, gains_beyond = [], []
    for m in range(members):
        mine = jnp.sum(jnp.where(iota((bank, total_z), 0) == ids[m], prof[...], 0.0), axis=0, keepdims=True)
        gains.append(1.0 + jnp.sum(jnp.where(here, mine, 0.0), axis=1, keepdims=True))
        gains_beyond.append([1.0 + jnp.sum(jnp.where(at, mine, 0.0), axis=1, keepdims=True) for at in beyond])

    loads[8].wait()
    z_at, y_at, x_at = iota((wz, ny), 0), iota((wz, ny), 1), iota((wx, ny), 0)
    for m in range(members):
        for x in (0, wx - 1, *range(1, wx - 1)):
            at = (m * wx + x) * wz
            rows = pl.ds(at, wz)
            c = now[rows, :]
            k = cour[pl.ds(x * wz, wz), :] * gains[m]
            coef[rows, :] = k
            lap = along_y(c, y_at) - 6.0 * c
            if x > 0:
                lap = lap + now[pl.ds(at - wz, wz), :]
            if x < wx - 1:
                lap = lap + now[pl.ds(at + wz, wz), :]
            lap = lap + jnp.where(z_at == 0, 0.0, pltpu.roll(c, 1, 0))
            lap = lap + jnp.where(z_at == wz - 1, 0.0, pltpu.roll(c, wz - 1, 0))
            nxt = (2.0 * c - prev[rows, :]) + k * lap
            if x == wx - 1:
                psend[0, m] = nxt
            elif x == 0:
                psend[1, m] = nxt
            else:
                one[rows, :] = nxt
            for b in range(2):
                zpsend[b, m, x : x + 1, :] = nxt[edge_z[b] : edge_z[b] + 1, :]
    for a in range(2):
        @pl.when(sends_box[a])
        def _(a=a):
            x_copies(a, parts)[0].start()
    for b in range(2):
        @pl.when(sends_slab[b])
        def _(b=b):
            z_copy(b, 1).start()

    for a in range(2):
        @pl.when(hears_box[1 - a])
        def _(a=a):
            pl.semaphore_wait(diag_sem.at[1 - a], 1)
            for b in range(2):
                @pl.when(sends_slab[b])
                def _(b=b):
                    corner_copy(a, b).start()

    loads[9].wait()

    def where_is(face):
        cell = cells[pl.ds(face, 1), :]
        cx = quotient(cell, total_z * ny)
        rest = cell - cx * (total_z * ny)
        cz = quotient(rest, ny)
        return cx - box * wx, cz - slab * wz, rest - cz * ny

    def hot(n, at):
        return jnp.where(iota((n, pts), 0) == at, 1.0, 0.0).astype(BF16)

    tall_x, tall_z = wx + 2 * MARGIN, wz + 2 * MARGIN
    px, pz, py = where_is(face_x)
    row_x[...] = hot(tall_z, jnp.where((px >= 0) & (px < wx), pz + MARGIN, -1))
    hot_x[...] = hot(ny, py)
    px, pz, py = where_is(jnp.where(slab == 0, 2, 3))
    row_z[...] = hot(tall_x, jnp.where((pz >= 0) & (pz < wz), px + MARGIN, -1))
    hot_z[...] = hot(ny, py)
    for face, row_hot, hot_at in ((4, row_low, hot_low), (5, row_high, hot_high)):
        px, pz, py = where_is(face)
        row_hot[...] = hot(tall_z, pz + MARGIN)
        hot_at[...] = hot(WIDE, px + MARGIN)

    for a in range(2):
        @pl.when(hears_box[a])
        def _(a=a):
            for c in x_copies(a, given):
                c.wait_recv()
    for a in range(2):
        plane = edge_x[1 - a]
        for m in range(members):
            rows = pl.ds((m * wx + plane) * wz, wz)
            ghost = jnp.where(hears_box[a], xghost[a, m], 0.0)
            one[rows, :] = psend[1 - a, m] + coef[rows, :] * ghost
    for b in range(2):
        @pl.when(hears_slab[b])
        def _(b=b):
            z_copy(b, 0).wait_recv()
            row = edge_z[1 - b]
            for m in range(members):
                for x in range(wx):
                    at = pl.ds((m * wx + x) * wz + row, 1)
                    one[at, :] += coef[at, :] * zghost[b, m, x : x + 1, :]

    for a in range(2):
        for b in range(2):
            @pl.when(hears_box[a] & hears_slab[b])
            def _(a=a, b=b):
                corner_copy(a, b).wait_recv()
    for b in range(2):
        @pl.when(hears_slab[b])
        def _(b=b):
            z_copy(b, 1).wait_recv()
    for a in range(2):
        @pl.when(hears_box[a])
        def _(a=a):
            x_copies(a, parts)[0].wait_recv()

    def across(a, b, m):
        return jnp.where(hears_box[a] & hears_slab[b], corner[a, b, m : m + 1, :], 0.0)

    for a in range(2):
        for m in range(members):
            beside = now[pl.ds((m * wx + edge_x[1 - a]) * wz, wz), :]
            beside = beside + jnp.where(z_at == 0, across(a, 0, m), 0.0)
            beside = beside + jnp.where(z_at == wz - 1, across(a, 1, m), 0.0)
            xout[a, m] = jnp.where(hears_box[a], xpart[a, m] + xcour[a] * gains[m] * beside, 0.0)
    for b in range(2):
        for m in range(members):
            beside = zsend[1 - b, m]
            beside = beside + jnp.where(x_at == 0, across(0, b, m), 0.0)
            beside = beside + jnp.where(x_at == wx - 1, across(1, b, m), 0.0)
            zout[b, m] = jnp.where(hears_slab[b], zpart[b, m] + zghost[b, members] * gains_beyond[m][b] * beside, 0.0)

    for d in range(1, n_slab):
        give(d, 0).wait_recv()

    @pl.when(box_edge)
    def _():
        for d in range(1, n_slab):
            give(d, 1).wait_recv()

    @pl.when(slab_edge)
    def _():
        for d in range(1, n_slab):
            give(d, 2).wait_recv()

    values_y, values_x, values_z = ysend[...], xvsend[...], zvsend[jnp.where(slab == 0, 0, 1)]
    for d in range(1, n_slab):
        values_y = values_y + yrecv[d - 1]
        values_x = values_x + xvrecv[d - 1]
        values_z = values_z + zvrecv[d - 1]
    values_x = jnp.where(box_edge, values_x, 0.0)
    values_z = jnp.where(slab_edge, values_z, 0.0)

    def rows_of(v, k):
        return [v[k + t : k + t + 1] for t in both]

    low_y = place(row_low, rows_of(values_y, 0), hot_low)
    high_y = place(row_high, rows_of(values_y, steps), hot_high)
    on_z = place(row_z, rows_of(values_z, 0), hot_z)
    on_x = place(row_x, rows_of(values_x, 0), hot_x)
    plane_x = jnp.where(box == 0, 0, wx - 1)
    line_z = jnp.where(slab == 0, 0, wz - 1)
    tiles = ny // 128

    def source(t, x, k, first, count):
        rows = slice(first + MARGIN, first + MARGIN + count)
        lanes = slice(k * 128, (k + 1) * 128)
        at = x + MARGIN
        lane = iota((count, 128), 1)
        out = jnp.where(iota((count, 128), 0) + first == line_z, on_z[t][at : at + 1, lanes], 0.0)
        if k == 0:
            out = out + jnp.where(lane == 0, low_y[t][rows, at : at + 1], 0.0)
        if k == tiles - 1:
            out = out + jnp.where(lane == 127, high_y[t][rows, at : at + 1], 0.0)
        if x in (0, wx - 1):
            out = out + jnp.where(plane_x == x, on_x[t][rows, lanes], 0.0)
        return out

    for k in range(tiles):
        lanes = slice(k * 128, (k + 1) * 128)
        for x in range(wx):
            plane = source(0, x, k, -MARGIN, tall_z)
            for b, row in ((0, MARGIN - 1), (1, MARGIN + wz)):
                line = plane[row : row + 1]
                for m in range(members):
                    zout[b, m, x : x + 1, lanes] += line
            for m in range(members):
                one[pl.ds((m * wx + x) * wz, wz), lanes] += plane[MARGIN : MARGIN + wz]
            src[pl.ds(x * wz, wz), lanes] = source(1, x, k, 0, wz)
        for a, x in ((0, -1), (1, wx)):
            plane = source(0, x, k, 0, wz)
            for m in range(members):
                xout[a, m, :, lanes] += plane

    for a in range(2):
        @pl.when(sends_box[a])
        def _(a=a):
            for c in x_copies(a, (*given, *parts)):
                c.wait_send()
            for b in range(2):
                @pl.when(sends_slab[b])
                def _(b=b):
                    corner_copy(a, b).wait_send()
    for b in range(2):
        @pl.when(sends_slab[b])
        def _(b=b):
            for i in range(2):
                z_copy(b, i).wait_send()
    each_give(lambda c: c.wait_send())


def last_kernel(dims, one, now, coef, xout, zout, src, next_h, last_h, two, sem):
    members, wx, wz, ny = dims[:4]
    group = 4 if wx % 4 == 0 else 1
    parts = wx // group
    last = pltpu.make_async_copy(one, last_h, sem.at[members * parts])
    last.start()
    z_at, y_at = iota((wz, ny), 0), iota((wz, ny), 1)

    def put(m, g):
        rows = pl.ds((m * wx + g * group) * wz, group * wz)
        return pltpu.make_async_copy(two.at[rows], next_h.at[rows], sem.at[m * parts + g])

    for m in range(members):
        for x in range(wx):
            at = (m * wx + x) * wz
            rows = pl.ds(at, wz)
            c = one[rows, :]
            lap = along_y(c, y_at) - 6.0 * c
            lap = lap + (one[pl.ds(at - wz, wz), :] if x > 0 else xout[0, m])
            lap = lap + (one[pl.ds(at + wz, wz), :] if x < wx - 1 else xout[1, m])
            lap = lap + jnp.where(z_at == 0, zout[0, m, x : x + 1, :], pltpu.roll(c, 1, 0))
            lap = lap + jnp.where(z_at == wz - 1, zout[1, m, x : x + 1, :], pltpu.roll(c, wz - 1, 0))
            two[rows, :] = (2.0 * c - now[rows, :]) + coef[rows, :] * lap + src[pl.ds(x * wz, wz), :]
            if x % group == group - 1:
                put(m, x // group).start()
    last.wait()
    for m in range(members):
        for g in range(parts):
            put(m, g).wait()


def on_device(pressure_now, pressure_prev, courant_sq, member_profiles, member_ids, stored_slabs,
              slab_home, interp_weights, surface_cells):
    members, wx, wz, ny = pressure_now.shape
    slots, length, points = stored_slabs.shape
    pts = surface_cells.shape[1]
    n_box, n_slab = lax.axis_size("box"), lax.axis_size("slab")
    dims = (members, wx, wz, ny, slots, length, pts, n_box, n_slab)
    rows = members * wx * wz
    peers = n_slab - 1
    tall_x, tall_z = wx + 2 * MARGIN, wz + 2 * MARGIN
    vmem = pl.BlockSpec(memory_space=pltpu.VMEM)
    in_hbm = lambda a: pltpu.with_memory_space_constraint(a, pltpu.HBM)
    hbm = pl.BlockSpec(memory_space=pltpu.HBM)
    struct = lambda *shape: jax.ShapeDtypeStruct(shape, F32)
    f32 = lambda *shape: pltpu.VMEM(shape, F32)
    bf16 = lambda *shape: pltpu.VMEM(shape, BF16)
    dma = pltpu.SemaphoreType.DMA
    kept = pl.pallas_call(
        functools.partial(kernel, dims),
        out_shape=(struct(rows, ny), struct(rows, ny), struct(rows, ny),
                   struct(2, members, wz, ny), struct(2, members, wx, ny), struct(wx * wz, ny)),
        in_specs=[pl.BlockSpec(memory_space=pltpu.SMEM)] + [hbm] * 8,
        out_specs=(vmem,) * 6,
        scratch_shapes=[
            pltpu.SMEM(member_ids.shape, I32),
            pltpu.VMEM(member_profiles.shape, F32), pltpu.VMEM(interp_weights.shape, F32),
            pltpu.VMEM(surface_cells.shape, I32),
            f32(rows, ny), f32(wx * wz, ny),
            f32(slots * length, 2 * pts), f32(slots * length, 2 * pts), f32(slots * length, pts),
            f32(2, members, wz, ny), f32(2, members + 1, wx, ny), f32(2, members, wx, ny), f32(2, 2, members, ny),
            f32(2, members, wz, ny), f32(2, wz, ny), f32(2, members, wz, ny),
            f32(2, members + 1, wx, ny), f32(2, members, wx, ny), f32(2, 2, members, ny),
            bf16(tall_z, pts), bf16(tall_x, pts), bf16(tall_z, pts), bf16(tall_z, pts),
            bf16(ny, pts), bf16(ny, pts), bf16(WIDE, pts), bf16(WIDE, pts),
            f32(4, pts), f32(2, pts), f32(2, 2, pts),
            f32(peers, 4, pts), f32(peers, 2, pts), f32(peers, 2, pts),
            dma((10,)), dma((4, members + 2)), dma((4, members + 2)), dma((2, 2)), dma((2, 2)),
            dma((peers, 3)), dma((peers, 3)), pltpu.SemaphoreType.REGULAR((2,)),
        ],
        compiler_params=pltpu.CompilerParams(collective_id=0, has_side_effects=True,
                                             vmem_limit_bytes=32 * 1024 * 1024),
    )(slab_home, *(in_hbm(a) for a in (
        member_ids, member_profiles, interp_weights, surface_cells,
        pressure_now.reshape(rows, ny), pressure_prev.reshape(rows, ny),
        courant_sq.reshape(wx * wz, ny), stored_slabs.reshape(slots * length, points),
    )))
    placed = pltpu.HBM((rows, ny), F32)
    new, last = pl.pallas_call(
        functools.partial(last_kernel, dims),
        out_shape=(placed, placed),
        in_specs=[vmem] * 6,
        out_specs=(hbm, hbm),
        scratch_shapes=[f32(rows, ny), dma((members * wx + 1,))],
        compiler_params=pltpu.CompilerParams(vmem_limit_bytes=4 * 1024 * 1024),
    )(*kept)
    return new.reshape(pressure_now.shape), last.reshape(pressure_now.shape)


def solution(mesh):
    in_specs = (
        P("ens", "box", "slab", None), P("ens", "box", "slab", None), P("box", "slab", None), P(),
        P("ens"), P("slab", None, None), P("ens"), P(), P(),
    )
    out_specs = (P("ens", "box", "slab", None), P("ens", "box", "slab", None))
    return jax.shard_map(on_device, mesh=mesh, in_specs=in_specs, out_specs=out_specs, check_vma=False)
```

time: 13 us -> 12.4 us (0.954)
  the two profiles are of different devices: /device:TPU:0 before, /device:TPU:1 now
where the time goes in v1:
time: 12.4 us; the launch traced here: 12.3 us
  Pallas kernels  11 us (89%)
  between operations  1.29 us (10%)
    pallas_call x1, Pallas kernels, on_device(): pl.pallas_call(functools.partial(kernel, dims), out_shape=(struct(rows, n...  9.64 us
    pallas_call x1, Pallas kernels, on_device(): pl.pallas_call(functools.partial(last_kernel, dims), out_shape=(placed, p...  1.35 us

profile of v1, /device:TPU:1, one launch (start us, length us, event | category | flops | bytes accessed | tf_op | source)
XLA Modules:
  0.0 12.3 jit_solution(14670431145763510294)
XLA Ops:
  1.3 9.6 %shard_map.104 = (f32[512,256]{1,0:T(8,128)S(1)}, f32[512,256]{1,0:T(8,128)S(1)}, f32[512,256]{1,0:T(8,128)S(1)}, f32[2,2,16,256]{3,2,1,0:T(8,128)S(1)}, f32[2,2...) custom-call(s32[1]{0:T(128)S(6)} %copy.11.home, s32[2]{0:T(128)} %ids_h.1, f32[8,64]{1,0:T(8,128)} %prof_h.1, ...), custom_call_target="tpu_custom_call" | custom-call | tf_op jit(solution)/shard_map/pallas_call | solution.py:437
  10.9 1.3 %shard_map.105 = (f32[512,256]{1,0:T(8,128)}, f32[512,256]{1,0:T(8,128)}) custom-call(f32[512,256]{1,0:T(8,128)S(1)} %get-tuple-element.10.one, f32[512,256]{1,0:T(8,128)S(1)} %get-tuple-element.11.now, f32[512,256]{1,0:T(8,128)S(1)} %get-tuple-element.12.coef, f32[2,2,16,256]{3,2,1,0:T(8,128)S(1)} %get-tuple-element.13.xout, ...), custom_call_target="tpu_custom_call" | custom-call | tf_op jit(solution)/shard_map/pallas_call | solution.py:467

commit v2 on v1

--- a/solution.py
+++ b/solution.py
@@ -66,8 +66,6 @@
         (slabs_h.at[:, pl.ds(pl.multiple_of(face_x * pts, 128), pts)], slab_x),
         (now_h, now), (cour_h, cour), (prof_h, prof), (ids_h, ids), (prev_h, prev), (cells_h, cells))
     loads = [pltpu.make_async_copy(src_, dst, load_sem.at[i]) for i, (src_, dst) in enumerate(pairs)]
-    for c in loads[:4]:
-        c.start()
 
     barrier = pltpu.get_barrier_semaphore()
 
@@ -86,7 +84,7 @@
         @pl.when(sends_box[a])
         def _(a=a):
             greet({"box": box + shift[a]})
-    for c in loads[4:]:
+    for c in loads:
         c.start()
 
     for i in range(4):
@@ -163,6 +161,15 @@
         return pltpu.make_async_remote_copy(
             csend.at[a, b], corner.at[a, b], cs_sem.at[a, b], cr_sem.at[a, b],
             device_id={"box": box + shift[a], "slab": slab + shift[b]}, device_id_type=MESH)
+
+    def send_corners(a):
+        @pl.when(sends_box[a])
+        def _():
+            pl.semaphore_wait(diag_sem.at[1 - a], 1)
+            for b in range(2):
+                @pl.when(sends_slab[b])
+                def _(b=b):
+                    corner_copy(a, b).start()
 
     box_peers = jnp.where(box > 0, 1, 0) + jnp.where(box < n_box - 1, 1, 0)
     pl.semaphore_wait(barrier, n_slab - 1 + box_peers)
@@ -214,6 +221,7 @@
                 one[rows, :] = nxt
             for b in range(2):
                 zpsend[b, m, x : x + 1, :] = nxt[edge_z[b] : edge_z[b] + 1, :]
+    send_corners(1)
     for a in range(2):
         @pl.when(sends_box[a])
         def _(a=a):
@@ -222,15 +230,6 @@
         @pl.when(sends_slab[b])
         def _(b=b):
             z_copy(b, 1).start()
-
-    for a in range(2):
-        @pl.when(hears_box[1 - a])
-        def _(a=a):
-            pl.semaphore_wait(diag_sem.at[1 - a], 1)
-            for b in range(2):
-                @pl.when(sends_slab[b])
-                def _(b=b):
-                    corner_copy(a, b).start()
 
     loads[9].wait()
 
@@ -256,6 +255,37 @@
         row_hot[...] = hot(tall_z, pz + MARGIN)
         hot_at[...] = hot(WIDE, px + MARGIN)
 
+    send_corners(0)
+
+
+    for d in range(1, n_slab):
+        give(d, 0).wait_recv()
+
+    @pl.when(box_edge)
+    def _():
+        for d in range(1, n_slab):
+            give(d, 1).wait_recv()
+
+    @pl.when(slab_edge)
+    def _():
+        for d in range(1, n_slab):
+            give(d, 2).wait_recv()
+
+    values_y, values_x, values_z = ysend[...], xvsend[...], zvsend[jnp.where(slab == 0, 0, 1)]
+    for d in range(1, n_slab):
+        values_y = values_y + yrecv[d - 1]
+        values_x = values_x + xvrecv[d - 1]
+        values_z = values_z + zvrecv[d - 1]
+    values_x = jnp.where(box_edge, values_x, 0.0)
+    values_z = jnp.where(slab_edge, values_z, 0.0)
+
+    def rows_of(v, k):
+        return [v[k + t : k + t + 1] for t in both]
+
+    low_y = place(row_low, rows_of(values_y, 0), hot_low)
+    high_y = place(row_high, rows_of(values_y, steps), hot_high)
+    on_z = place(row_z, rows_of(values_z, 0), hot_z)
+    on_x = place(row_x, rows_of(values_x, 0), hot_x)
     for a in range(2):
         @pl.when(hears_box[a])
         def _(a=a):
@@ -307,34 +337,6 @@
             beside = beside + jnp.where(x_at == wx - 1, across(1, b, m), 0.0)
             zout[b, m] = jnp.where(hears_slab[b], zpart[b, m] + zghost[b, members] * gains_beyond[m][b] * beside, 0.0)
 
-    for d in range(1, n_slab):
-        give(d, 0).wait_recv()
-
-    @pl.when(box_edge)
-    def _():
-        for d in range(1, n_slab):
-            give(d, 1).wait_recv()
-
-    @pl.when(slab_edge)
-    def _():
-        for d in range(1, n_slab):
-            give(d, 2).wait_recv()
-
-    values_y, values_x, values_z = ysend[...], xvsend[...], zvsend[jnp.where(slab == 0, 0, 1)]
-    for d in range(1, n_slab):
-        values_y = values_y + yrecv[d - 1]
-        values_x = values_x + xvrecv[d - 1]
-        values_z = values_z + zvrecv[d - 1]
-    values_x = jnp.where(box_edge, values_x, 0.0)
-    values_z = jnp.where(slab_edge, values_z, 0.0)
-
-    def rows_of(v, k):
-        return [v[k + t : k + t + 1] for t in both]
-
-    low_y = place(row_low, rows_of(values_y, 0), hot_low)
-    high_y = place(row_high, rows_of(values_y, steps), hot_high)
-    on_z = place(row_z, rows_of(values_z, 0), hot_z)
-    on_x = place(row_x, rows_of(values_x, 0), hot_x)
     plane_x = jnp.where(box == 0, 0, wx - 1)
     line_z = jnp.where(slab == 0, 0, wz - 1)
     tiles = ny // 128

time: 12.4 us -> 11.2 us (0.903)
  the two profiles are of different devices: /device:TPU:1 before, /device:TPU:0 now
where the time goes in v2:
time: 11.2 us; the launch traced here: 11.1 us
  Pallas kernels  9.79 us (87%)
  between operations  1.29 us (12%)
    pallas_call x1, Pallas kernels, on_device(): pl.pallas_call(functools.partial(kernel, dims), out_shape=(struct(rows, n...  8.44 us
    pallas_call x1, Pallas kernels, on_device(): pl.pallas_call(functools.partial(last_kernel, dims), out_shape=(placed, p...  1.35 us

profile of v2, /device:TPU:0, one launch (start us, length us, event | category | flops | bytes accessed | tf_op | source)
XLA Modules:
  0.0 11.1 jit_solution(12775429696831697819)
XLA Ops:
  1.3 8.4 %shard_map.104 = (f32[512,256]{1,0:T(8,128)S(1)}, f32[512,256]{1,0:T(8,128)S(1)}, f32[512,256]{1,0:T(8,128)S(1)}, f32[2,2,16,256]{3,2,1,0:T(8,128)S(1)}, f32[2,2...) custom-call(s32[1]{0:T(128)S(6)} %copy.11.home, s32[2]{0:T(128)} %ids_h.1, f32[8,64]{1,0:T(8,128)} %prof_h.1, ...), custom_call_target="tpu_custom_call" | custom-call | tf_op jit(solution)/shard_map/pallas_call | solution.py:439
  9.7 1.3 %shard_map.105 = (f32[512,256]{1,0:T(8,128)}, f32[512,256]{1,0:T(8,128)}) custom-call(f32[512,256]{1,0:T(8,128)S(1)} %get-tuple-element.10.one, f32[512,256]{1,0:T(8,128)S(1)} %get-tuple-element.11.now, f32[512,256]{1,0:T(8,128)S(1)} %get-tuple-element.12.coef, f32[2,2,16,256]{3,2,1,0:T(8,128)S(1)} %get-tuple-element.13.xout, ...), custom_call_target="tpu_custom_call" | custom-call | tf_op jit(solution)/shard_map/pallas_call | solution.py:469

commit v3 on v2

--- a/solution.py
+++ b/solution.py
@@ -52,7 +52,7 @@
            psend, zsend, zpsend, csend, xghost, xcour, xpart, zghost, zpart, corner,
            row_x, row_z, row_low, row_high, hot_x, hot_z, hot_low, hot_high,
            ysend, xvsend, zvsend, yrecv, xvrecv, zvrecv,
-           load_sem, hs_sem, hr_sem, cs_sem, cr_sem, vs_sem, vr_sem, diag_sem):
+           load_sem, hs_sem, hr_sem, cs_sem, cr_sem, vs_sem, vr_sem, here_sem, peer_sem):
     members, wx, wz, ny, slots, length, pts, n_box, n_slab = dims
     steps = 2
     block = wx * wz
@@ -78,14 +78,41 @@
     hears_slab = (slab > 0, slab < n_slab - 1)
     shift = (1, -1)
 
-    for d in range(1, n_slab):
-        greet({"slab": lax.rem(slab + d, n_slab)})
-    for a in range(2):
-        @pl.when(sends_box[a])
-        def _(a=a):
-            greet({"box": box + shift[a]})
+    @pl.when(sends_box[0])
+    def _():
+        greet({"box": box + 1})
+
+    @pl.when(sends_box[0] & sends_slab[0])
+    def _():
+        greet({"box": box + 1, "slab": slab + 1})
+
+    for d in range(1, n_slab):
+        @pl.when(slab + d < n_slab)
+        def _(d=d):
+            greet({"slab": slab + d})
     for c in loads:
         c.start()
+    lower_box = jnp.where(box > 0, 1, 0)
+
+    @pl.when((box > 0) | (slab > 0))
+    def _():
+        pl.semaphore_wait(barrier, slab + lower_box * jnp.where(slab > 0, 2, 1))
+
+    def tell(ref, target):
+        pl.semaphore_signal(ref, inc=1, device_id=target, device_id_type=MESH)
+
+    @pl.when(sends_box[1])
+    def _():
+        tell(here_sem.at[0], {"box": box - 1})
+
+    for d in range(1, n_slab):
+        @pl.when(slab >= d)
+        def _(d=d):
+            tell(peer_sem.at[d - 1], {"slab": slab - d})
+
+    @pl.when(sends_box[1] & sends_slab[1])
+    def _():
+        tell(here_sem.at[1], {"box": box - 1, "slab": slab - 1})
 
     for i in range(4):
         loads[i].wait()
@@ -132,17 +159,6 @@
         peer = lax.rem(slab + d, n_slab)
         return (None, box_edge, peer == 0, peer == n_slab - 1)[kind]
 
-    def each_give(act):
-        for d in range(1, n_slab):
-            for kind in range(4):
-                cond = gives(d, kind)
-                if cond is None:
-                    act(give(d, kind))
-                else:
-                    @pl.when(cond)
-                    def _(d=d, kind=kind):
-                        act(give(d, kind))
-
     given, parts = range(members + 1), range(members + 1, members + 2)
 
     def x_copies(a, which):
@@ -162,28 +178,33 @@
             csend.at[a, b], corner.at[a, b], cs_sem.at[a, b], cr_sem.at[a, b],
             device_id={"box": box + shift[a], "slab": slab + shift[b]}, device_id_type=MESH)
 
-    def send_corners(a):
-        @pl.when(sends_box[a])
-        def _():
-            pl.semaphore_wait(diag_sem.at[1 - a], 1)
-            for b in range(2):
-                @pl.when(sends_slab[b])
-                def _(b=b):
-                    corner_copy(a, b).start()
-
-    box_peers = jnp.where(box > 0, 1, 0) + jnp.where(box < n_box - 1, 1, 0)
-    pl.semaphore_wait(barrier, n_slab - 1 + box_peers)
-    for a in range(2):
-        @pl.when(sends_box[a])
-        def _(a=a):
-            pl.semaphore_signal(diag_sem.at[a], inc=1, device_id={"box": box + shift[a]}, device_id_type=MESH)
-            for c in x_copies(a, given):
-                c.start()
-    each_give(lambda c: c.start())
-    for b in range(2):
-        @pl.when(sends_slab[b])
-        def _(b=b):
-            z_copy(b, 0).start()
+    def give_all(d, act):
+        for kind in range(4):
+            cond = gives(d, kind)
+            if cond is None:
+                act(give(d, kind))
+            else:
+                @pl.when(cond)
+                def _(kind=kind):
+                    act(give(d, kind))
+
+    for d in range(1, n_slab):
+        @pl.when(slab + d >= n_slab)
+        def _(d=d):
+            give_all(d, lambda c: c.start())
+
+    @pl.when(sends_box[1])
+    def _():
+        for c in x_copies(1, given):
+            c.start()
+
+    @pl.when(sends_slab[1])
+    def _():
+        z_copy(1, 0).start()
+
+    @pl.when(sends_box[1] & sends_slab[1])
+    def _():
+        corner_copy(1, 1).start()
 
     loads[6].wait()
     loads[7].wait()
@@ -221,15 +242,41 @@
                 one[rows, :] = nxt
             for b in range(2):
                 zpsend[b, m, x : x + 1, :] = nxt[edge_z[b] : edge_z[b] + 1, :]
-    send_corners(1)
-    for a in range(2):
-        @pl.when(sends_box[a])
-        def _(a=a):
-            x_copies(a, parts)[0].start()
-    for b in range(2):
-        @pl.when(sends_slab[b])
-        def _(b=b):
-            z_copy(b, 1).start()
+    @pl.when(sends_box[1])
+    def _():
+        x_copies(1, parts)[0].start()
+
+    @pl.when(sends_slab[1])
+    def _():
+        z_copy(1, 1).start()
+
+    for d in range(1, n_slab):
+        @pl.when(slab + d < n_slab)
+        def _(d=d):
+            pl.semaphore_wait(peer_sem.at[d - 1], 1)
+            give_all(d, lambda c: c.start())
+            if d == 1:
+                for i in range(2):
+                    z_copy(0, i).start()
+
+                @pl.when(sends_box[1])
+                def _():
+                    corner_copy(1, 0).start()
+
+    @pl.when(sends_box[0])
+    def _():
+        pl.semaphore_wait(here_sem.at[0], 1)
+        for c in x_copies(0, (*given, *parts)):
+            c.start()
+
+        @pl.when(sends_slab[1])
+        def _():
+            corner_copy(0, 1).start()
+
+    @pl.when(sends_box[0] & sends_slab[0])
+    def _():
+        pl.semaphore_wait(here_sem.at[1], 1)
+        corner_copy(0, 0).start()
 
     loads[9].wait()
 
@@ -254,8 +301,6 @@
         px, pz, py = where_is(face)
         row_hot[...] = hot(tall_z, pz + MARGIN)
         hot_at[...] = hot(WIDE, px + MARGIN)
-
-    send_corners(0)
 
 
     for d in range(1, n_slab):
@@ -385,7 +430,8 @@
         def _(b=b):
             for i in range(2):
                 z_copy(b, i).wait_send()
-    each_give(lambda c: c.wait_send())
+    for d in range(1, n_slab):
+        give_all(d, lambda c: c.wait_send())
 
 
 def last_kernel(dims, one, now, coef, xout, zout, src, next_h, last_h, two, sem):
@@ -456,7 +502,7 @@
             f32(4, pts), f32(2, pts), f32(2, 2, pts),
             f32(peers, 4, pts), f32(peers, 2, pts), f32(peers, 2, pts),
             dma((10,)), dma((4, members + 2)), dma((4, members + 2)), dma((2, 2)), dma((2, 2)),
-            dma((peers, 3)), dma((peers, 3)), pltpu.SemaphoreType.REGULAR((2,)),
+            dma((peers, 3)), dma((peers, 3)), pltpu.SemaphoreType.REGULAR((2,)), pltpu.SemaphoreType.REGULAR((peers,)),
         ],
         compiler_params=pltpu.CompilerParams(collective_id=0, has_side_effects=True,
                                              vmem_limit_bytes=32 * 1024 * 1024),

time: 11.2 us -> 11 us (0.982)
  Pallas kernels: 9.79 us -> 9.52 us
    pallas_call x1, Pallas kernels: 8.44 us -> 8.17 us  [on_device(): pl.pallas_call(functools.partial(kernel, dims), out_shape=(struct(rows, n...]
where the time goes in v3:
time: 11 us; the launch traced here: 10.8 us
  Pallas kernels  9.52 us (87%)
  between operations  1.29 us (12%)
    pallas_call x1, Pallas kernels, on_device(): pl.pallas_call(functools.partial(kernel, dims), out_shape=(struct(rows, n...  8.17 us
    pallas_call x1, Pallas kernels, on_device(): pl.pallas_call(functools.partial(last_kernel, dims), out_shape=(placed, p...  1.35 us

profile of v3, /device:TPU:0, one launch (start us, length us, event | category | flops | bytes accessed | tf_op | source)
XLA Modules:
  0.0 10.8 jit_solution(1125484467262136405)
XLA Ops:
  1.3 8.2 %shard_map.104 = (f32[512,256]{1,0:T(8,128)S(1)}, f32[512,256]{1,0:T(8,128)S(1)}, f32[512,256]{1,0:T(8,128)S(1)}, f32[2,2,16,256]{3,2,1,0:T(8,128)S(1)}, f32[2,2...) custom-call(s32[1]{0:T(128)S(6)} %copy.11.home, s32[2]{0:T(128)} %ids_h.1, f32[8,64]{1,0:T(8,128)} %prof_h.1, ...), custom_call_target="tpu_custom_call" | custom-call | tf_op jit(solution)/shard_map/pallas_call | solution.py:485
  9.5 1.3 %shard_map.105 = (f32[512,256]{1,0:T(8,128)}, f32[512,256]{1,0:T(8,128)}) custom-call(f32[512,256]{1,0:T(8,128)S(1)} %get-tuple-element.10.one, f32[512,256]{1,0:T(8,128)S(1)} %get-tuple-element.11.now, f32[512,256]{1,0:T(8,128)S(1)} %get-tuple-element.12.coef, f32[2,2,16,256]{3,2,1,0:T(8,128)S(1)} %get-tuple-element.13.xout, ...), custom_call_target="tpu_custom_call" | custom-call | tf_op jit(solution)/shard_map/pallas_call | solution.py:515

commit v4 on v3

--- a/solution.py
+++ b/solution.py
@@ -9,7 +9,7 @@
 
 F32, BF16, I32 = jnp.float32, jnp.bfloat16, jnp.int32
 MESH = pl.DeviceIdType.MESH
-MARGIN, WIDE = 8, 128
+MARGIN = 8
 
 
 def iota(shape, dim):
@@ -51,7 +51,7 @@
            ids, prof, weights, cells, prev, cour, slab_y, slab_z, slab_x,
            psend, zsend, zpsend, csend, xghost, xcour, xpart, zghost, zpart, corner,
            row_x, row_z, row_low, row_high, hot_x, hot_z, hot_low, hot_high,
-           ysend, xvsend, zvsend, yrecv, xvrecv, zvrecv,
+           ysend, xvsend, zvsend, yrecv, xvrecv, zvrecv, xadd, zadd,
            load_sem, hs_sem, hr_sem, cs_sem, cr_sem, vs_sem, vr_sem, here_sem, peer_sem):
     members, wx, wz, ny, slots, length, pts, n_box, n_slab = dims
     steps = 2
@@ -135,6 +135,33 @@
         zvsend[f] = jnp.concatenate([offered(slab_z, f * pts, t) for t in both], axis=0)
     xvsend[...] = jnp.concatenate([offered(slab_x, 0, t) for t in both], axis=0)
 
+    def give(d, kind):
+        peer = lax.rem(slab + d, n_slab)
+        ref, into = ((ysend, yrecv), (xvsend, xvrecv), (zvsend.at[0], zvrecv), (zvsend.at[1], zvrecv))[kind]
+        k = min(kind, 2)
+        return pltpu.make_async_remote_copy(
+            ref, into.at[d - 1], vs_sem.at[d - 1, k], vr_sem.at[d - 1, k],
+            device_id={"slab": peer}, device_id_type=MESH)
+
+    def gives(d, kind):
+        peer = lax.rem(slab + d, n_slab)
+        return (None, box_edge, peer == 0, peer == n_slab - 1)[kind]
+
+    def give_all(d, act):
+        for kind in range(4):
+            cond = gives(d, kind)
+            if cond is None:
+                act(give(d, kind))
+            else:
+                @pl.when(cond)
+                def _(kind=kind):
+                    act(give(d, kind))
+
+    for d in range(1, n_slab):
+        @pl.when(slab + d >= n_slab)
+        def _(d=d):
+            give_all(d, lambda c: c.start())
+
     loads[4].wait()
     loads[5].wait()
     edge_x, edge_z = (wx - 1, 0), (wz - 1, 0)
@@ -147,18 +174,6 @@
             for m in range(members):
                 csend[a, b, m : m + 1, :] = now[pl.ds((m * wx + edge_x[a]) * wz + edge_z[b], 1), :]
 
-    def give(d, kind):
-        peer = lax.rem(slab + d, n_slab)
-        ref, into = ((ysend, yrecv), (xvsend, xvrecv), (zvsend.at[0], zvrecv), (zvsend.at[1], zvrecv))[kind]
-        k = min(kind, 2)
-        return pltpu.make_async_remote_copy(
-            ref, into.at[d - 1], vs_sem.at[d - 1, k], vr_sem.at[d - 1, k],
-            device_id={"slab": peer}, device_id_type=MESH)
-
-    def gives(d, kind):
-        peer = lax.rem(slab + d, n_slab)
-        return (None, box_edge, peer == 0, peer == n_slab - 1)[kind]
-
     given, parts = range(members + 1), range(members + 1, members + 2)
 
     def x_copies(a, which):
@@ -177,21 +192,6 @@
         return pltpu.make_async_remote_copy(
             csend.at[a, b], corner.at[a, b], cs_sem.at[a, b], cr_sem.at[a, b],
             device_id={"box": box + shift[a], "slab": slab + shift[b]}, device_id_type=MESH)
-
-    def give_all(d, act):
-        for kind in range(4):
-            cond = gives(d, kind)
-            if cond is None:
-                act(give(d, kind))
-            else:
-                @pl.when(cond)
-                def _(kind=kind):
-                    act(give(d, kind))
-
-    for d in range(1, n_slab):
-        @pl.when(slab + d >= n_slab)
-        def _(d=d):
-            give_all(d, lambda c: c.start())
 
     @pl.when(sends_box[1])
     def _():
@@ -300,8 +300,25 @@
     for face, row_hot, hot_at in ((4, row_low, hot_low), (5, row_high, hot_high)):
         px, pz, py = where_is(face)
         row_hot[...] = hot(tall_z, pz + MARGIN)
-        hot_at[...] = hot(WIDE, px + MARGIN)
-
+        hot_at[...] = hot(tall_x, px + MARGIN)
+
+
+    for a in range(2):
+        @pl.when(sends_box[a])
+        def _(a=a):
+            for c in x_copies(a, (*given, *parts)):
+                c.wait_send()
+            for b in range(2):
+                @pl.when(sends_slab[b])
+                def _(b=b):
+                    corner_copy(a, b).wait_send()
+    for b in range(2):
+        @pl.when(sends_slab[b])
+        def _(b=b):
+            for i in range(2):
+                z_copy(b, i).wait_send()
+    for d in range(1, n_slab):
+        give_all(d, lambda c: c.wait_send())
 
     for d in range(1, n_slab):
         give(d, 0).wait_recv()
@@ -352,6 +369,37 @@
                     at = pl.ds((m * wx + x) * wz + row, 1)
                     one[at, :] += coef[at, :] * zghost[b, m, x : x + 1, :]
 
+    plane_x = jnp.where(box == 0, 0, wx - 1)
+    line_z = jnp.where(slab == 0, 0, wz - 1)
+    tiles = ny // 128
+
+    def source(t, x, k, first, count):
+        rows = slice(first + MARGIN, first + MARGIN + count)
+        lanes = slice(k * 128, (k + 1) * 128)
+        at = x + MARGIN
+        lane = iota((count, 128), 1)
+        out = jnp.where(iota((count, 128), 0) + first == line_z, on_z[t][at : at + 1, lanes], 0.0)
+        if k == 0:
+            out = out + jnp.where(lane == 0, low_y[t][rows, at : at + 1], 0.0)
+        if k == tiles - 1:
+            out = out + jnp.where(lane == 127, high_y[t][rows, at : at + 1], 0.0)
+        if x in (0, wx - 1):
+            out = out + jnp.where(plane_x == x, on_x[t][rows, lanes], 0.0)
+        return out
+
+    for k in range(tiles):
+        lanes = slice(k * 128, (k + 1) * 128)
+        for x in range(wx):
+            plane = source(0, x, k, -MARGIN, tall_z)
+            for b, row in ((0, MARGIN - 1), (1, MARGIN + wz)):
+                line = plane[row : row + 1]
+                zadd[b, x : x + 1, lanes] = line
+            for m in range(members):
+                one[pl.ds((m * wx + x) * wz, wz), lanes] += plane[MARGIN : MARGIN + wz]
+            src[pl.ds(x * wz, wz), lanes] = source(1, x, k, 0, wz)
+        for a, x in ((0, -1), (1, wx)):
+            xadd[a, :, lanes] = source(0, x, k, 0, wz)
+
     for a in range(2):
         for b in range(2):
             @pl.when(hears_box[a] & hears_slab[b])
@@ -374,64 +422,13 @@
             beside = now[pl.ds((m * wx + edge_x[1 - a]) * wz, wz), :]
             beside = beside + jnp.where(z_at == 0, across(a, 0, m), 0.0)
             beside = beside + jnp.where(z_at == wz - 1, across(a, 1, m), 0.0)
-            xout[a, m] = jnp.where(hears_box[a], xpart[a, m] + xcour[a] * gains[m] * beside, 0.0)
+            xout[a, m] = jnp.where(hears_box[a], (xpart[a, m] + xadd[a]) + xcour[a] * gains[m] * beside, 0.0)
     for b in range(2):
         for m in range(members):
             beside = zsend[1 - b, m]
             beside = beside + jnp.where(x_at == 0, across(0, b, m), 0.0)
             beside = beside + jnp.where(x_at == wx - 1, across(1, b, m), 0.0)
-            zout[b, m] = jnp.where(hears_slab[b], zpart[b, m] + zghost[b, members] * gains_beyond[m][b] * beside, 0.0)
-
-    plane_x = jnp.where(box == 0, 0, wx - 1)
-    line_z = jnp.where(slab == 0, 0, wz - 1)
-    tiles = ny // 128
-
-    def source(t, x, k, first, count):
-        rows = slice(first + MARGIN, first + MARGIN + count)
-        lanes = slice(k * 128, (k + 1) * 128)
-        at = x + MARGIN
-        lane = iota((count, 128), 1)
-        out = jnp.where(iota((count, 128), 0) + first == line_z, on_z[t][at : at + 1, lanes], 0.0)
-        if k == 0:
-            out = out + jnp.where(lane == 0, low_y[t][rows, at : at + 1], 0.0)
-        if k == tiles - 1:
-            out = out + jnp.where(lane == 127, high_y[t][rows, at : at + 1], 0.0)
-        if x in (0, wx - 1):
-            out = out + jnp.where(plane_x == x, on_x[t][rows, lanes], 0.0)
-        return out
-
-    for k in range(tiles):
-        lanes = slice(k * 128, (k + 1) * 128)
-        for x in range(wx):
-            plane = source(0, x, k, -MARGIN, tall_z)
-            for b, row in ((0, MARGIN - 1), (1, MARGIN + wz)):
-                line = plane[row : row + 1]
-                for m in range(members):
-                    zout[b, m, x : x + 1, lanes] += line
-            for m in range(members):
-                one[pl.ds((m * wx + x) * wz, wz), lanes] += plane[MARGIN : MARGIN + wz]
-            src[pl.ds(x * wz, wz), lanes] = source(1, x, k, 0, wz)
-        for a, x in ((0, -1), (1, wx)):
-            plane = source(0, x, k, 0, wz)
-            for m in range(members):
-                xout[a, m, :, lanes] += plane
-
-    for a in range(2):
-        @pl.when(sends_box[a])
-        def _(a=a):
-            for c in x_copies(a, (*given, *parts)):
-                c.wait_send()
-            for b in range(2):
-                @pl.when(sends_slab[b])
-                def _(b=b):
-                    corner_copy(a, b).wait_send()
-    for b in range(2):
-        @pl.when(sends_slab[b])
-        def _(b=b):
-            for i in range(2):
-                z_copy(b, i).wait_send()
-    for d in range(1, n_slab):
-        give_all(d, lambda c: c.wait_send())
+            zout[b, m] = jnp.where(hears_slab[b], (zpart[b, m] + zadd[b]) + zghost[b, members] * gains_beyond[m][b] * beside, 0.0)
 
 
 def last_kernel(dims, one, now, coef, xout, zout, src, next_h, last_h, two, sem):
@@ -498,9 +495,10 @@
             f32(2, members, wz, ny), f32(2, wz, ny), f32(2, members, wz, ny),
             f32(2, members + 1, wx, ny), f32(2, members, wx, ny), f32(2, 2, members, ny),
             bf16(tall_z, pts), bf16(tall_x, pts), bf16(tall_z, pts), bf16(tall_z, pts),
-            bf16(ny, pts), bf16(ny, pts), bf16(WIDE, pts), bf16(WIDE, pts),
+            bf16(ny, pts), bf16(ny, pts), bf16(tall_x, pts), bf16(tall_x, pts),
             f32(4, pts), f32(2, pts), f32(2, 2, pts),
             f32(peers, 4, pts), f32(peers, 2, pts), f32(peers, 2, pts),
+            f32(2, wz, ny), f32(2, wx, ny),
             dma((10,)), dma((4, members + 2)), dma((4, members + 2)), dma((2, 2)), dma((2, 2)),
             dma((peers, 3)), dma((peers, 3)), pltpu.SemaphoreType.REGULAR((2,)), pltpu.SemaphoreType.REGULAR((peers,)),
         ],

time: 11 us -> 10.8 us (0.982)
  Pallas kernels: 9.52 us -> 9.34 us
    pallas_call x1, Pallas kernels: 8.17 us -> 7.99 us  [on_device(): pl.pallas_call(functools.partial(kernel, dims), out_shape=(struct(rows, n...]
where the time goes in v4:
time: 10.8 us; the launch traced here: 10.6 us
  Pallas kernels  9.34 us (86%)
  between operations  1.29 us (12%)
    pallas_call x1, Pallas kernels, on_device(): pl.pallas_call(functools.partial(kernel, dims), out_shape=(struct(rows, n...  7.99 us
    pallas_call x1, Pallas kernels, on_device(): pl.pallas_call(functools.partial(last_kernel, dims), out_shape=(placed, p...  1.35 us

profile of v4, /device:TPU:0, one launch (start us, length us, event | category | flops | bytes accessed | tf_op | source)
XLA Modules:
  0.0 10.6 jit_solution(14300107246202026677)
XLA Ops:
  1.3 8.0 %shard_map.104 = (f32[512,256]{1,0:T(8,128)S(1)}, f32[512,256]{1,0:T(8,128)S(1)}, f32[512,256]{1,0:T(8,128)S(1)}, f32[2,2,16,256]{3,2,1,0:T(8,128)S(1)}, f32[2,2...) custom-call(s32[1]{0:T(128)S(6)} %copy.11.home, s32[2]{0:T(128)} %ids_h.1, f32[8,64]{1,0:T(8,128)} %prof_h.1, ...), custom_call_target="tpu_custom_call" | custom-call | tf_op jit(solution)/shard_map/pallas_call | solution.py:482
  9.3 1.3 %shard_map.105 = (f32[512,256]{1,0:T(8,128)}, f32[512,256]{1,0:T(8,128)}) custom-call(f32[512,256]{1,0:T(8,128)S(1)} %get-tuple-element.10.one, f32[512,256]{1,0:T(8,128)S(1)} %get-tuple-element.11.now, f32[512,256]{1,0:T(8,128)S(1)} %get-tuple-element.12.coef, f32[2,2,16,256]{3,2,1,0:T(8,128)S(1)} %get-tuple-element.13.xout, ...), custom_call_target="tpu_custom_call" | custom-call | tf_op jit(solution)/shard_map/pallas_call | solution.py:513

commit v5 on v4

--- a/solution.py
+++ b/solution.py
@@ -147,8 +147,8 @@
         peer = lax.rem(slab + d, n_slab)
         return (None, box_edge, peer == 0, peer == n_slab - 1)[kind]
 
-    def give_all(d, act):
-        for kind in range(4):
+    def give_all(d, act, kinds=range(4)):
+        for kind in kinds:
             cond = gives(d, kind)
             if cond is None:
                 act(give(d, kind))
@@ -157,10 +157,11 @@
                 def _(kind=kind):
                     act(give(d, kind))
 
-    for d in range(1, n_slab):
-        @pl.when(slab + d >= n_slab)
-        def _(d=d):
-            give_all(d, lambda c: c.start())
+    for kinds in ((0,), (1, 2, 3)):
+        for d in range(1, n_slab):
+            @pl.when(slab + d >= n_slab)
+            def _(d=d, kinds=kinds):
+                give_all(d, lambda c: c.start(), kinds)
 
     loads[4].wait()
     loads[5].wait()
@@ -323,6 +324,16 @@
     for d in range(1, n_slab):
         give(d, 0).wait_recv()
 
+    values_y = ysend[...]
+    for d in range(1, n_slab):
+        values_y = values_y + yrecv[d - 1]
+
+    def rows_of(v, k):
+        return [v[k + t : k + t + 1] for t in both]
+
+    low_y = place(row_low, rows_of(values_y, 0), hot_low)
+    high_y = place(row_high, rows_of(values_y, steps), hot_high)
+
     @pl.when(box_edge)
     def _():
         for d in range(1, n_slab):
@@ -333,19 +344,13 @@
         for d in range(1, n_slab):
             give(d, 2).wait_recv()
 
-    values_y, values_x, values_z = ysend[...], xvsend[...], zvsend[jnp.where(slab == 0, 0, 1)]
-    for d in range(1, n_slab):
-        values_y = values_y + yrecv[d - 1]
+    values_x, values_z = xvsend[...], zvsend[jnp.where(slab == 0, 0, 1)]
+    for d in range(1, n_slab):
         values_x = values_x + xvrecv[d - 1]
         values_z = values_z + zvrecv[d - 1]
     values_x = jnp.where(box_edge, values_x, 0.0)
     values_z = jnp.where(slab_edge, values_z, 0.0)
 
-    def rows_of(v, k):
-        return [v[k + t : k + t + 1] for t in both]
-
-    low_y = place(row_low, rows_of(values_y, 0), hot_low)
-    high_y = place(row_high, rows_of(values_y, steps), hot_high)
     on_z = place(row_z, rows_of(values_z, 0), hot_z)
     on_x = place(row_x, rows_of(values_x, 0), hot_x)
     for a in range(2):

time: 10.8 us -> 10.8 us (level)
  no operation moved by 1% of the time
where the time goes in v5:
time: 10.8 us; the launch traced here: 10.6 us
  Pallas kernels  9.36 us (87%)
  between operations  1.29 us (12%)
    pallas_call x1, Pallas kernels, on_device(): pl.pallas_call(functools.partial(kernel, dims), out_shape=(struct(rows, n...  8.01 us
    pallas_call x1, Pallas kernels, on_device(): pl.pallas_call(functools.partial(last_kernel, dims), out_shape=(placed, p...  1.35 us

profile of v5, /device:TPU:0, one launch (start us, length us, event | category | flops | bytes accessed | tf_op | source)
XLA Modules:
  0.0 10.6 jit_solution(8609803778250689656)
XLA Ops:
  1.3 8.0 %shard_map.104 = (f32[512,256]{1,0:T(8,128)S(1)}, f32[512,256]{1,0:T(8,128)S(1)}, f32[512,256]{1,0:T(8,128)S(1)}, f32[2,2,16,256]{3,2,1,0:T(8,128)S(1)}, f32[2,2...) custom-call(s32[1]{0:T(128)S(6)} %copy.11.home, s32[2]{0:T(128)} %ids_h.1, f32[8,64]{1,0:T(8,128)} %prof_h.1, ...), custom_call_target="tpu_custom_call" | custom-call | tf_op jit(solution)/shard_map/pallas_call | solution.py:487
  9.3 1.3 %shard_map.105 = (f32[512,256]{1,0:T(8,128)}, f32[512,256]{1,0:T(8,128)}) custom-call(f32[512,256]{1,0:T(8,128)S(1)} %get-tuple-element.10.one, f32[512,256]{1,0:T(8,128)S(1)} %get-tuple-element.11.now, f32[512,256]{1,0:T(8,128)S(1)} %get-tuple-element.12.coef, f32[2,2,16,256]{3,2,1,0:T(8,128)S(1)} %get-tuple-element.13.xout, ...), custom_call_target="tpu_custom_call" | custom-call | tf_op jit(solution)/shard_map/pallas_call | solution.py:518
